TPU v7x, 32 devices: a whole 2x2x4 slice. The times are simulated.
32 devices in a mesh: ep: 4 (over y, x), fsdp: 8 (over z, core).
Axes of the slice: x: 2, y: 2, z: 4, core: 2. Of those that a mesh axis runs over, the one named last changes fastest.
Arguments:
- w_gate: float32 [64, 2048, 1024], P('ep', 'fsdp'), may hold values from -0.1875 to 0.1875
- avg_gate: bfloat16 [64, 2048, 1024], P('ep', 'fsdp'), may hold values from -0.0625 to 0.0625
- w_up: float32 [64, 2048, 1024], P('ep', 'fsdp'), may hold values from -0.1875 to 0.1875
- avg_up: bfloat16 [64, 2048, 1024], P('ep', 'fsdp'), may hold values from -0.0625 to 0.0625
- w_down: float32 [64, 1024, 2048], P('ep', None, 'fsdp'), may hold values from -0.25 to 0.25
- avg_down: bfloat16 [64, 1024, 2048], P('ep', None, 'fsdp'), may hold values from -0.09375 to 0.09375
- router_weight: float32 [2048, 64], P('fsdp', 'ep'), may hold values from -0.125 to 0.125
- router_gain: float32 [2048], P('fsdp'), may hold values from 0.25 to 1.75
Outputs:
- serve_gate: bfloat16 [64, 2048, 1024], P('ep', None, 'fsdp')
- serve_up: bfloat16 [64, 2048, 1024], P('ep', None, 'fsdp')
- serve_down: bfloat16 [64, 1024, 2048], P('ep', 'fsdp')
- scale_gate: float32 [64, 1024], P('ep', 'fsdp')
- scale_up: float32 [64, 1024], P('ep', 'fsdp')
- scale_down: float32 [64, 1024], P('ep', 'fsdp')
- serve_router: bfloat16 [2048, 64], replicated
All inputs are finite; a program needn't handle non-finite values.
Results may differ from a plain program's by a relative error of at most 0.001.
Values may be sent and summed in bfloat16 or wider, within the bound.
A program may use at most 192 MiB of HBM per device.

v0:
```python
import jax
import jax.numpy as jnp
from jax import lax
from jax.sharding import PartitionSpec as P


def on_device(w_gate, avg_gate, w_up, avg_up, w_down, avg_down, router_weight, router_gain):
    fresh_gate = w_gate + avg_gate.astype(jnp.float32)
    fresh_up = w_up + avg_up.astype(jnp.float32)
    fresh_down = w_down + avg_down.astype(jnp.float32)
    total_gate, total_up, total_down = lax.psum(
        (
            jnp.sum(fresh_gate * fresh_gate, axis=1),
            jnp.sum(fresh_up * fresh_up, axis=1),
            jnp.sum(fresh_down * fresh_down, axis=2),
        ),
        "fsdp",
    )
    scale_gate = jnp.sqrt(total_gate)
    scale_up = jnp.sqrt(total_up)
    scale_down = jnp.sqrt(total_down)
    narrow_gate, narrow_up, narrow_down = (
        (fresh_gate / jnp.expand_dims(scale_gate, 1)).astype(jnp.bfloat16),
        (fresh_up / jnp.expand_dims(scale_up, 1)).astype(jnp.bfloat16),
        (fresh_down / jnp.expand_dims(scale_down, 2)).astype(jnp.bfloat16),
    )
    serve_gate, serve_up = (
        lax.all_to_all(narrow_gate, "fsdp", split_axis=2, concat_axis=1, tiled=True),
        lax.all_to_all(narrow_up, "fsdp", split_axis=2, concat_axis=1, tiled=True),
    )
    serve_down = lax.all_to_all(narrow_down, "fsdp", split_axis=1, concat_axis=2, tiled=True)
    scale_gate = lax.dynamic_slice_in_dim(
        scale_gate, lax.axis_index("fsdp") * serve_gate.shape[2], serve_gate.shape[2], axis=1
    )
    scale_up = lax.dynamic_slice_in_dim(
        scale_up, lax.axis_index("fsdp") * serve_up.shape[2], serve_up.shape[2], axis=1
    )
    scale_down = lax.dynamic_slice_in_dim(
        scale_down, lax.axis_index("fsdp") * serve_down.shape[1], serve_down.shape[1], axis=1
    )
    part_router = (router_weight * router_gain[:, None]).astype(jnp.bfloat16)
    row_router = lax.all_gather(part_router, "fsdp", axis=0, tiled=True)
    serve_router = lax.all_gather(row_router, "ep", axis=1, tiled=True)
    return (serve_gate, serve_up, serve_down, scale_gate, scale_up, scale_down, serve_router)


def solution(mesh):
    placed = (
        P("ep", "fsdp", None),
        P("ep", "fsdp", None),
        P("ep", "fsdp", None),
        P("ep", "fsdp", None),
        P("ep", None, "fsdp"),
        P("ep", None, "fsdp"),
        P("fsdp", "ep"),
        P("fsdp"),
    )
    return jax.shard_map(
        on_device,
        mesh=mesh,
        in_specs=placed,
        out_specs=(
            P("ep", None, "fsdp"),
            P("ep", None, "fsdp"),
            P("ep", "fsdp", None),
            P("ep", "fsdp"),
            P("ep", "fsdp"),
            P("ep", "fsdp"),
            P(),
        ),
        check_vma=False,
    )
```

profile of v0, /device:TPU:0, one launch (start us, length us, event | category | flops | bytes accessed | tf_op | source)
XLA Modules:
  0.0 824.8 jit_solution(4685212397091970850)
XLA Ops:
  7.2 17.6 %copy.31 = f32[16,256,1024]{1,0,2:T(8,128)} copy(f32[16,256,1024]{2,1,0:T(8,128)} %param.8) | data formatting | bytes 33554432 | tf_op args[0]
  24.8 17.6 %copy.34 = f32[16,256,1024]{1,0,2:T(8,128)} copy(f32[16,256,1024]{2,1,0:T(8,128)} %param.10) | data formatting | bytes 33554432 | tf_op args[2]
  42.4 12.5 %copy.30 = bf16[16,256,1024]{1,0,2:T(8,128)(2,1)} copy(bf16[16,256,1024]{2,1,0:T(8,128)(2,1)} %param.9) | data formatting | bytes 16777216 | tf_op args[1]
  54.9 12.5 %copy.33 = bf16[16,256,1024]{1,0,2:T(8,128)(2,1)} copy(bf16[16,256,1024]{2,1,0:T(8,128)(2,1)} %param.11) | data formatting | bytes 16777216 | tf_op args[3]
  67.4 25.2 %multiply_reduce_fusion = f32[16,1024]{0,1:T(8,128)} fusion(f32[16,1024,256]{2,1,0:T(8,128)} %param.12, bf16[16,1024,256]{2,1,0:T(8,128)(2,1)} %param.13), kind=kLoop, calls=%fused_computation.2 | loop fusion | flops 16760832 | bytes 25231360 | tf_op jit(solution)/shard_map/reduce_sum | solution.py:15
  92.6 13.2 %multiply_reduce_fusion.1 = (f32[16,1024]{0,1:T(8,128)}, f32[16,1024]{0,1:T(8,128)}) fusion(f32[16,256,1024]{1,0,2:T(8,128)} %copy.34, bf16[16,256,1024]{1,0,2:T(8,128)(2,1)S(1)} %copy-done.1, f32[16,256,1024]{1,0,2:T(8,128)} %copy.31, bf16[16,256,1024]{1,0,2:T(8,128)(2,1)S(1)} %copy-done), kind=kLoop, calls=%fused_computation.4 | loop fusion | flops 33521664 | bytes 50462720 | tf_op jit(solution)/shard_map/reduce_sum | solution.py:14
  105.8 65.1 %all-reduce.3.cloned.1.call-done = (f32[16,1024]{0,1:T(8,128)}, f32[16,1024]{0,1:T(8,128)}, f32[16,1024]{0,1:T(8,128)}) async-done(((f32[16,1024]{0,1:T(8,128)}, f32[16,1024]{0,1:T(8,128)}, f32[16,1024]{0,1:T(8,128)}), (f32[16,1024]{0,1:T(8,128)}, f32[16,1024]{0,1:T(8,128)}, f32[16,1024]{0,1:T(8,128)})) %all-reduce.3.cloned.1.call-update) | async-done | bytes 196624 | tf_op jit(solution)/shard_map/psum | solution.py:11
  170.9 1.2 sqrt.10
  172.1 12.0 %divide_convert_fusion.1 = bf16[16,256,1024]{1,0,2:T(8,128)(2,1)} fusion(f32[16,256,1024]{1,0,2:T(8,128)} %copy.34, bf16[16,256,1024]{1,0,2:T(8,128)(2,1)} %copy.33, f32[16,1024]{0,1:T(8,128)S(1)} %sqrt.10), kind=kLoop, calls=%fused_computation.3 | loop fusion | flops 16777216 | bytes 33619968 | tf_op jit(solution)/shard_map/convert_element_type | solution.py:24
  184.1 5.1 all-to-all-start.1
  189.3 12.0 %divide_convert_fusion.2 = bf16[16,256,1024]{1,0,2:T(8,128)(2,1)} fusion(f32[16,256,1024]{1,0,2:T(8,128)} %copy.31, bf16[16,256,1024]{1,0,2:T(8,128)(2,1)} %copy.30, f32[16,1024]{0,1:T(8,128)S(1)} %sqrt.9), kind=kLoop, calls=%fused_computation.6 | loop fusion | flops 16777216 | bytes 33619968 | tf_op jit(solution)/shard_map/convert_element_type | solution.py:23
  201.3 171.7 %all-to-all-done.1 = bf16[16,256,1024]{1,0,2:T(8,128)(2,1)} async-done(((bf16[16,256,1024]{1,0,2:T(8,128)(2,1)}), bf16[16,256,1024]{1,0,2:T(8,128)(2,1)}, u32[]{:S(2)}, u32[]{:S(2)}) %all-to-all-start.1) | async-done | bytes 8388640 | tf_op jit(solution)/shard_map/all_to_all | solution.py:29
  373.0 5.1 all-to-all-start
  378.3 23.8 %divide_convert_fusion = bf16[16,1024,256]{2,0,1:T(8,128)(2,1)} fusion(f32[16,1024,256]{2,1,0:T(8,128)} %param.12, f32[16,1024]{0,1:T(8,128)S(1)} %sqrt.11, bf16[16,1024,256]{2,1,0:T(8,128)(2,1)} %param.13), kind=kLoop, calls=%fused_computation.1 | loop fusion | flops 16777216 | bytes 33619968 | tf_op jit(solution)/shard_map/convert_element_type | solution.py:25
  402.1 159.8 %all-to-all-done = bf16[16,256,1024]{1,0,2:T(8,128)(2,1)} async-done(((bf16[16,256,1024]{1,0,2:T(8,128)(2,1)}), bf16[16,256,1024]{1,0,2:T(8,128)(2,1)}, u32[]{:S(2)}, u32[]{:S(2)}) %all-to-all-start) | async-done | bytes 8388640 | tf_op jit(solution)/shard_map/all_to_all | solution.py:28
  561.8 5.0 all-to-all-start.2
  566.9 189.9 %all_gather.6 = bf16[2048,16]{0,1:T(8,128)(2,1)S(1)} all-gather(bf16[256,16]{0,1:T(8,128)(2,1)S(1)} %multiply_convert_fusion), channel_id=1, replica_groups=mesh['ep'=4,'fsdp'=8] {'fsdp'}, dimensions={0}, use_global_device_ids=true | all-gather | bytes 73728 | tf_op jit(solution)/shard_map/all_gather | solution.py:42
  756.8 9.1 %all_gather.7 = bf16[2048,64]{0,1:T(8,128)(2,1)S(1)} all-gather(bf16[2048,16]{0,1:T(8,128)(2,1)S(1)} %all_gather.6), channel_id=1, replica_groups=mesh['ep'=4,'fsdp'=8] {'ep'}, dimensions={1}, use_global_device_ids=true | all-gather | bytes 327680 | tf_op jit(solution)/shard_map/all_gather | solution.py:43
  765.9 0.7 copy.39
  767.9 12.3 %copy.35 = bf16[16,8,256,128]{3,2,1,0:T(8,128)(2,1)} copy(bf16[16,8,256,128]{2,0,3,1:T(8,128)(2,1)} %bitcast.4) | data formatting | bytes 16777216 | tf_op jit(solution)/shard_map/all_to_all | solution.py:29
  780.2 12.3 %copy.32 = bf16[16,8,256,128]{3,2,1,0:T(8,128)(2,1)} copy(bf16[16,8,256,128]{2,0,3,1:T(8,128)(2,1)} %bitcast.1) | data formatting | bytes 16777216 | tf_op jit(solution)/shard_map/all_to_all | solution.py:28
  792.5 11.4 %copy.38 = bf16[16,128,8,256]{3,2,1,0:T(8,128)(2,1)} copy(bf16[16,128,8,256]{3,0,1,2:T(8,128)(2,1)} %bitcast.7) | data formatting | bytes 16777216 | tf_op jit(solution)/shard_map/all_to_all | solution.py:31
  803.9 13.4 %all_to_all.50 = bf16[16,128,2048]{2,1,0:T(8,128)(2,1)} reshape(bf16[16,128,8,256]{3,2,1,0:T(8,128)(2,1)} %copy.38) | data formatting | bytes 16777216 | tf_op jit(solution)/shard_map/all_to_all | solution.py:31
  817.3 0.7 copy.53
  (23 shorter events, 1.7 us)
Async XLA Ops:
  7.2 163.7 %all-reduce.3.cloned.1.call-start = ((), (), s32[]{:S(2)}) async-start(), calls=%async_computation.3 | async-start | bytes 3145728 | tf_op jit(solution)/shard_map/psum | solution.py:11
  67.4 25.2 %copy-start = (bf16[16,256,1024]{1,0,2:T(8,128)(2,1)S(1)}, bf16[16,256,1024]{1,0,2:T(8,128)(2,1)}, u32[]{:S(2)}) copy-start(bf16[16,256,1024]{1,0,2:T(8,128)(2,1)} %copy.30) | copy-start | bytes 25165828
  67.4 25.2 %copy-start.1 = (bf16[16,256,1024]{1,0,2:T(8,128)(2,1)S(1)}, bf16[16,256,1024]{1,0,2:T(8,128)(2,1)}, u32[]{:S(2)}) copy-start(bf16[16,256,1024]{1,0,2:T(8,128)(2,1)} %copy.33) | copy-start | bytes 25165828
  184.1 5.1 copy-start.3
  184.1 189.0 %all-to-all-start.1 = ((bf16[16,256,1024]{1,0,2:T(8,128)(2,1)}), bf16[16,256,1024]{1,0,2:T(8,128)(2,1)}, u32[]{:S(2)}, u32[]{:S(2)}) async-start(bf16[16,256,1024]{1,0,2:T(8,128)(2,1)} %divide_convert_fusion.1), calls=%async_computation.1 | async-start | bytes 16777216 | tf_op jit(solution)/shard_map/all_to_all | solution.py:29
  201.3 176.9 %copy-start.2 = (f32[16,1024]{0,1:T(8,128)S(1)}, f32[16,1024]{0,1:T(8,128)}, u32[]{:S(2)}) copy-start(f32[16,1024]{0,1:T(8,128)} %get-tuple-element.16) | copy-start | bytes 196612
  373.0 188.8 %all-to-all-start = ((bf16[16,256,1024]{1,0,2:T(8,128)(2,1)}), bf16[16,256,1024]{1,0,2:T(8,128)(2,1)}, u32[]{:S(2)}, u32[]{:S(2)}) async-start(bf16[16,256,1024]{1,0,2:T(8,128)(2,1)} %divide_convert_fusion.2), calls=%async_computation | async-start | bytes 16777216 | tf_op jit(solution)/shard_map/all_to_all | solution.py:28
  402.1 164.8 %copy-start.4 = (f32[256,16]{0,1:T(8,128)S(1)}, f32[256,16]{0,1:T(8,128)}, u32[]{:S(2)}) copy-start(f32[256,16]{0,1:T(8,128)} %param.14) | copy-start | bytes 49156
  402.1 164.8 %copy-start.5 = (f32[256]{0:T(256)S(1)}, f32[256]{0:T(256)}, u32[]{:S(2)}) copy-start(f32[256]{0:T(256)} %param.15) | copy-start | bytes 3076
  561.8 230.7 %all-to-all-start.2 = ((bf16[16,1024,256]{2,0,1:T(8,128)(2,1)}), bf16[16,1024,256]{2,0,1:T(8,128)(2,1)}, u32[]{:S(2)}, u32[]{:S(2)}) async-start(bf16[16,1024,256]{2,0,1:T(8,128)(2,1)} %divide_convert_fusion), calls=%async_computation.2 | async-start | bytes 16777216 | tf_op jit(solution)/shard_map/all_to_all | solution.py:31
Sparse Core Ops, SparseCore 0:
  105.9 64.9 all-reduce.2
where the time goes:
time: 827 us; the launch traced here: 825 us
  waiting for transfers between devices  397 us (48%)
  blocking collectives  199 us (24%)
  local copies, waits for them, and re-layouts  114 us (14%)
  other arithmetic  86.1 us (10%)
  starting transfers between devices  15.3 us (2%)
  between operations  14.1 us (2%)
    all_gather x1, blocking collectives, on_device(): row_router = lax.all_gather(part_router, 'fsdp', axis=0, tiled=True)  190 us
    all_to_all x1, waiting for transfers between devices, on_device(): lax.all_to_all(narrow_up, 'fsdp', split_axis=2, concat_axis=1, tiled=True)  172 us
    all_to_all x1, waiting for transfers between devices, on_device(): lax.all_to_all(narrow_gate, 'fsdp', split_axis=2, concat_axis=1, tiled=True)  160 us
    psum x1, waiting for transfers between devices, on_device(): lax.psum((jnp.sum(fresh_gate * fresh_gate, axis=1), jnp.sum(fresh_up * fr...  65.1 us
    unnamed x20, local copies, waits for them, and re-layouts  62.9 us
    reduce_sum x1, other arithmetic, on_device(): jnp.sum(fresh_down * fresh_down, axis=2)  25.2 us
    all_to_all x2, local copies, waits for them, and re-layouts, on_device(): lax.all_to_all(narrow_down, 'fsdp', split_axis=1, concat_axis=2, tiled=True)  24.8 us
    convert_element_type x1, other arithmetic, on_device(): (fresh_down / jnp.expand_dims(scale_down, 2)).astype(jnp.bfloat16)  23.8 us
  transfers between devices with their start and end apart: 4, of which 3 were waited for; matrix products, arithmetic and copies ran while one was open for 8% of the time, Pallas kernels for 0%

commit v1 on v0

v1 whole, which is shorter than its diff:
```python
import jax
import jax.numpy as jnp
from jax import lax
from jax.experimental import pallas as pl
from jax.sharding import PartitionSpec as P


def fresh_of(w, avg):
    return w + avg.astype(jnp.float32)


def narrow_of(w, avg, total, axis):
    return (fresh_of(w, avg) / jnp.expand_dims(jnp.sqrt(total), axis)).astype(jnp.bfloat16)


def squares(w, avg, axis):
    fresh = fresh_of(w, avg)
    return jnp.sum(fresh * fresh, axis=axis)


def exchange(x):
    return lax.all_to_all(x, "fsdp", split_axis=0, concat_axis=0, tiled=True)


def sum_kernel(w_ref, avg_ref, total_ref):
    fresh = w_ref[0] + avg_ref[0].astype(jnp.float32)
    total_ref[0] = jnp.sum(fresh * fresh, axis=0, keepdims=True)


def piece_kernel(n, w_ref, avg_ref, total_ref, out_ref):
    width = w_ref.shape[2] // n
    for k in range(n):
        at = slice(k * width, (k + 1) * width)
        fresh = w_ref[0, :, at] + avg_ref[0, :, at].astype(jnp.float32)
        out_ref[k, 0] = (fresh / jnp.sqrt(total_ref[0, :, at])).astype(jnp.bfloat16)


def column_squares(w, avg):
    experts, depth, width = w.shape
    block = pl.BlockSpec((1, depth, width), lambda e: (e, 0, 0))
    total = pl.pallas_call(
        sum_kernel,
        grid=(experts,),
        in_specs=[block, block],
        out_specs=pl.BlockSpec((1, 1, width), lambda e: (e, 0, 0)),
        out_shape=jax.ShapeDtypeStruct((experts, 1, width), jnp.float32),
        cost_estimate=pl.CostEstimate(flops=3 * w.size, bytes_accessed=6 * w.size, transcendentals=0),
    )(w, avg)
    return total.reshape(experts, width)


def column_pieces(w, avg, total):
    n = lax.axis_size("fsdp")
    experts, depth, width = w.shape
    block = pl.BlockSpec((1, depth, width), lambda e: (e, 0, 0))
    return pl.pallas_call(
        lambda *refs: piece_kernel(n, *refs),
        grid=(experts,),
        in_specs=[block, block, pl.BlockSpec((1, 1, width), lambda e: (e, 0, 0))],
        out_specs=pl.BlockSpec((n, 1, depth, width // n), lambda e: (0, e, 0, 0)),
        out_shape=jax.ShapeDtypeStruct((n, experts, depth, width // n), jnp.bfloat16),
        cost_estimate=pl.CostEstimate(flops=3 * w.size, bytes_accessed=8 * w.size, transcendentals=0),
    )(w, avg, total.reshape(experts, 1, width))


def columns(pieces):
    n, experts, depth, width = pieces.shape
    return exchange(pieces).transpose(1, 0, 2, 3).reshape(experts, n * depth, width)


def join_kernel(in_ref, out_ref):
    n, _, _, depth = in_ref.shape
    for k in range(n):
        out_ref[0, :, k * depth : (k + 1) * depth] = in_ref[k, 0]


def rows(x):
    n = lax.axis_size("fsdp")
    experts, height, depth = x.shape
    part = height // n
    pieces = exchange(x.reshape(experts, n, part, depth).transpose(1, 0, 2, 3))
    return pl.pallas_call(
        join_kernel,
        grid=(experts,),
        in_specs=[pl.BlockSpec((n, 1, part, depth), lambda e: (0, e, 0, 0))],
        out_specs=pl.BlockSpec((1, part, n * depth), lambda e: (e, 0, 0)),
        out_shape=jax.ShapeDtypeStruct((experts, part, n * depth), x.dtype),
        cost_estimate=pl.CostEstimate(flops=0, bytes_accessed=4 * x.size, transcendentals=0),
    )(pieces)


def on_device(w_gate, avg_gate, w_up, avg_up, w_down, avg_down, router_weight, router_gain):
    part_router = (router_weight * router_gain[:, None]).astype(jnp.bfloat16)
    row_router = lax.all_gather(part_router, "fsdp", axis=0, tiled=True)
    serve_router = lax.all_gather(row_router, "ep", axis=1, tiled=True)
    total_gate = lax.psum(column_squares(w_gate, avg_gate), "fsdp")
    total_gate, serve_router = lax.optimization_barrier((total_gate, serve_router))
    gate = column_pieces(w_gate, avg_gate, total_gate)
    gate, late_up, late_down = lax.optimization_barrier((gate, avg_up, avg_down))
    serve_gate = columns(gate)
    square_up, square_down = column_squares(w_up, late_up), squares(w_down, late_down, 2)
    total_up, total_down = lax.psum((square_up, square_down), "fsdp")
    up = column_pieces(w_up, avg_up, total_up)
    up, total_down = lax.optimization_barrier((up, total_down))
    serve_up = columns(up)
    serve_down = rows(narrow_of(w_down, avg_down, total_down, 2))

    def own(total, width):
        return jnp.sqrt(
            lax.dynamic_slice_in_dim(total, lax.axis_index("fsdp") * width, width, axis=1)
        )

    scale_gate = own(total_gate, serve_gate.shape[2])
    scale_up = own(total_up, serve_up.shape[2])
    scale_down = own(total_down, serve_down.shape[1])
    return (serve_gate, serve_up, serve_down, scale_gate, scale_up, scale_down, serve_router)


def solution(mesh):
    placed = (
        P("ep", "fsdp", None),
        P("ep", "fsdp", None),
        P("ep", "fsdp", None),
        P("ep", "fsdp", None),
        P("ep", None, "fsdp"),
        P("ep", None, "fsdp"),
        P("fsdp", "ep"),
        P("fsdp"),
    )
    return jax.shard_map(
        on_device,
        mesh=mesh,
        in_specs=placed,
        out_specs=(
            P("ep", None, "fsdp"),
            P("ep", None, "fsdp"),
            P("ep", "fsdp", None),
            P("ep", "fsdp"),
            P("ep", "fsdp"),
            P("ep", "fsdp"),
            P(),
        ),
        check_vma=False,
    )
```

time: 827 us -> 690 us (0.83)
  blocking collectives: 199 us -> 24.7 us
  waiting for transfers between devices: 397 us -> 504 us
  local copies, waits for them, and re-layouts: 114 us -> 32.8 us
  Pallas kernels: 0 us -> 75.9 us
  other arithmetic: 86.1 us -> 21.7 us
    all_gather x1, blocking collectives: 190 us -> 15.7 us  [on_device(): row_router = lax.all_gather(part_router, 'fsdp', axis=0, tiled=True)]
    all_to_all x3, waiting for transfers between devices: 331 us -> 413 us  [exchange(): return lax.all_to_all(x, 'fsdp', split_axis=0, concat_axis=0, tiled=True)]
    pallas_call x0 -> x5, Pallas kernels: none -> 75.9 us  [the longest x2 34 us: column_pieces(): pl.pallas_call(lambda *refs: piece_kernel(n, *refs), grid=(experts,), in_...]
    unnamed x20 -> x9, local copies, waits for them, and re-layouts: 62.9 us -> 3.68 us
    all_to_all x4 -> x0, local copies, waits for them, and re-layouts: 49.4 us -> none  [the longest x2 24.8 us: on_device(): lax.all_to_all(narrow_down, 'fsdp', split_axis=1, concat_axis=2, tiled=True)]
    convert_element_type x3 -> x1, other arithmetic: 47.7 us -> 12 us  [narrow_of(): (fresh_of(w, avg) / jnp.expand_dims(jnp.sqrt(total), axis)).astype(jnp.bf...]
    reduce_sum x2 -> x1, other arithmetic: 38.4 us -> 9.74 us  [squares(): return jnp.sum(fresh * fresh, axis=axis)]
    psum x1 -> x2, waiting for transfers between devices: 65.1 us -> 90.9 us  [the longest x1 58 us: on_device(): total_up, total_down = lax.psum((square_up, square_down), 'fsdp')]
  transfers between devices with their start and end apart: 4 -> 5, of which waited for: 3 -> 5; matrix products, arithmetic and copies ran while one was open for 8% -> 7% of each run, Pallas kernels for 0% -> 5%
where the time goes in v1:
time: 690 us; the launch traced here: 688 us
  waiting for transfers between devices  504 us (73%)
  Pallas kernels  75.9 us (11%)
  local copies, waits for them, and re-layouts  32.8 us (5%)
  blocking collectives  24.7 us (4%)
  other arithmetic  21.7 us (3%)
  starting transfers between devices  15 us (2%)
  between operations  14.1 us (2%)
    all_to_all x3, waiting for transfers between devices, exchange(): return lax.all_to_all(x, 'fsdp', split_axis=0, concat_axis=0, tiled=True)  413 us
    psum x1, waiting for transfers between devices, on_device(): total_up, total_down = lax.psum((square_up, square_down), 'fsdp')  58 us
    pallas_call x2, Pallas kernels, column_pieces(): pl.pallas_call(lambda *refs: piece_kernel(n, *refs), grid=(experts,), in_...  34 us
    psum x1, waiting for transfers between devices, on_device(): total_gate = lax.psum(column_squares(w_gate, avg_gate), 'fsdp')  32.9 us
    pallas_call x2, Pallas kernels, column_squares(): pl.pallas_call(sum_kernel, grid=(experts,), in_specs=[block, block], out_...  29.9 us
    transpose x2, local copies, waits for them, and re-layouts, columns(): exchange(pieces).transpose(1, 0, 2, 3).reshape(experts, n * depth, width)  15.8 us
    all_gather x1, blocking collectives, on_device(): row_router = lax.all_gather(part_router, 'fsdp', axis=0, tiled=True)  15.7 us
    all_to_all x3, starting transfers between devices, exchange(): return lax.all_to_all(x, 'fsdp', split_axis=0, concat_axis=0, tiled=True)  14.9 us
  transfers between devices with their start and end apart: 5, of which 5 were waited for; matrix products, arithmetic and copies ran while one was open for 7% of the time, Pallas kernels for 5%

profile of v1, /device:TPU:0, one launch (start us, length us, event | category | flops | bytes accessed | tf_op | source)
XLA Modules:
  0.0 688.3 jit_solution(17806020933095240582)
XLA Ops:
  7.2 14.9 %shard_map.135 = f32[16,1,1024]{2,1,0:T(1,128)} custom-call(f32[16,256,1024]{2,1,0:T(8,128)} %refs_0_.2, bf16[16,256,1024]{2,1,0:T(8,128)(2,1)} %refs_1_.2), custom_call_target="tpu_custom_call" | custom-call | flops 12582912 | bytes 25165824 | tf_op jit(solution)/shard_map/pallas_call | solution.py:41
  22.2 1.5 copy.25
  23.7 15.7 %all_gather.6 = bf16[2048,16]{0,1:T(8,128)(2,1)S(1)} all-gather(bf16[256,16]{0,1:T(8,128)(2,1)S(1)} %multiply_convert_fusion), channel_id=1, replica_groups=mesh['ep'=4,'fsdp'=8] {'fsdp'}, dimensions={0}, use_global_device_ids=true | all-gather | bytes 73728 | tf_op jit(solution)/shard_map/all_gather | solution.py:94
  39.4 9.0 %all_gather.7 = bf16[2048,64]{0,1:T(8,128)(2,1)S(1)} all-gather(bf16[2048,16]{0,1:T(8,128)(2,1)S(1)} %all_gather.6), channel_id=1, replica_groups=mesh['ep'=4,'fsdp'=8] {'ep'}, dimensions={1}, use_global_device_ids=true | all-gather | bytes 327680 | tf_op jit(solution)/shard_map/all_gather | solution.py:95
  48.4 32.9 %all-reduce.4.cloned.1.call-done = f32[16,1024]{1,0:T(8,128)} async-done(((f32[16,1024]{1,0:T(8,128)}), f32[16,1024]{1,0:T(8,128)}) %all-reduce.4.cloned.1.call-update) | async-done | bytes 65552 | tf_op jit(solution)/shard_map/psum | solution.py:96
  81.3 1.5 reshape.38.refs_2_
  82.8 17.0 %shard_map.136 = bf16[8,16,256,128]{3,2,1,0:T(8,128)(2,1)} custom-call(f32[16,256,1024]{2,1,0:T(8,128)} %refs_0_.2, bf16[16,256,1024]{2,1,0:T(8,128)(2,1)} %refs_1_.2, f32[16,1,1024]{2,1,0:T(1,128)} %reshape.38.refs_2_), custom_call_target="tpu_custom_call" | custom-call | flops 12582912 | bytes 33554432 | tf_op jit(solution)/shard_map/pallas_call | solution.py:56
  99.8 4.9 all-to-all-start
  104.8 14.9 %shard_map.137 = f32[16,1,1024]{2,1,0:T(1,128)} custom-call(f32[16,256,1024]{2,1,0:T(8,128)} %refs_0_.3, bf16[16,256,1024]{2,1,0:T(8,128)(2,1)} %refs_1_.3), custom_call_target="tpu_custom_call" | custom-call | flops 12582912 | bytes 25165824 | tf_op jit(solution)/shard_map/pallas_call | solution.py:41
  119.7 1.5 copy.24
  121.2 9.7 %multiply_reduce_fusion = f32[16,1024]{1,0:T(8,128)} fusion(f32[16,1024,256]{2,1,0:T(8,128)} %param.12, bf16[16,1024,256]{2,1,0:T(8,128)(2,1)} %param.13), kind=kLoop, calls=%fused_computation.1 | loop fusion | flops 16760832 | bytes 25231360 | tf_op jit(solution)/shard_map/reduce_sum | solution.py:18
  131.0 58.0 %all-reduce.6.cloned.1.call-done = (f32[16,1024]{1,0:T(8,128)}, f32[16,1024]{1,0:T(8,128)}) async-done(((f32[16,1024]{1,0:T(8,128)}, f32[16,1024]{1,0:T(8,128)}), (f32[16,1024]{1,0:T(8,128)}, f32[16,1024]{1,0:T(8,128)})) %all-reduce.6.cloned.1.call-update) | async-done | bytes 131088 | tf_op jit(solution)/shard_map/psum | solution.py:102
  189.0 1.5 reshape.41.refs_2_
  190.5 17.0 %shard_map.138 = bf16[8,16,256,128]{3,2,1,0:T(8,128)(2,1)} custom-call(f32[16,256,1024]{2,1,0:T(8,128)} %refs_0_.3, bf16[16,256,1024]{2,1,0:T(8,128)(2,1)} %refs_1_.3, f32[16,1,1024]{2,1,0:T(1,128)} %reshape.41.refs_2_), custom_call_target="tpu_custom_call" | custom-call | flops 12582912 | bytes 33554432 | tf_op jit(solution)/shard_map/pallas_call | solution.py:56
  207.5 83.5 %all-to-all-done = bf16[8,16,256,128]{3,2,1,0:T(8,128)(2,1)} async-done(((bf16[8,16,256,128]{3,2,1,0:T(8,128)(2,1)}), bf16[8,16,256,128]{3,2,1,0:T(8,128)(2,1)}, u32[]{:S(2)}, u32[]{:S(2)}) %all-to-all-start) | async-done | bytes 8388640 | tf_op jit(solution)/shard_map/all_to_all | solution.py:22
  291.0 5.0 all-to-all-start.1
  296.1 12.0 %divide_convert_fusion = bf16[16,1024,256]{2,1,0:T(8,128)(2,1)} fusion(f32[16,1024,256]{2,1,0:T(8,128)} %param.12, bf16[16,1024,256]{2,1,0:T(8,128)(2,1)} %param.13, f32[16,1024]{1,0:T(8,128)S(1)} %sqrt.12), kind=kLoop, calls=%fused_computation | loop fusion | flops 16777216 | bytes 33619968 | tf_op jit(solution)/shard_map/convert_element_type | solution.py:13
  308.1 7.7 %copy.23 = bf16[16,8,128,256]{3,2,0,1:T(8,128)(2,1)} copy(bf16[16,8,128,256]{3,2,1,0:T(8,128)(2,1)} %bitcast.15) | data formatting | bytes 16777216 | tf_op jit(solution)/shard_map/reshape | solution.py:81
  315.8 164.1 %all-to-all-done.1 = bf16[8,16,256,128]{3,2,1,0:T(8,128)(2,1)} async-done(((bf16[8,16,256,128]{3,2,1,0:T(8,128)(2,1)}), bf16[8,16,256,128]{3,2,1,0:T(8,128)(2,1)}, u32[]{:S(2)}, u32[]{:S(2)}) %all-to-all-start.1) | async-done | bytes 8388640 | tf_op jit(solution)/shard_map/all_to_all | solution.py:22
  479.9 4.9 all-to-all-start.2
  487.5 7.9 %copy.15 = bf16[16,8,256,128]{3,2,1,0:T(8,128)(2,1)} copy(bf16[16,8,256,128]{3,2,0,1:T(8,128)(2,1)} %bitcast) | data formatting | bytes 16777216 | tf_op jit(solution)/shard_map/transpose | solution.py:68
  495.4 7.9 %copy.16 = bf16[16,8,256,128]{3,2,1,0:T(8,128)(2,1)} copy(bf16[16,8,256,128]{3,2,0,1:T(8,128)(2,1)} %bitcast.2) | data formatting | bytes 16777216 | tf_op jit(solution)/shard_map/transpose | solution.py:68
  503.3 165.5 %all-to-all-done.2.in_ref = bf16[8,16,128,256]{3,2,1,0:T(8,128)(2,1)} async-done(((bf16[8,16,128,256]{3,2,1,0:T(8,128)(2,1)}), bf16[8,16,128,256]{3,2,1,0:T(8,128)(2,1)}, u32[]{:S(2)}, u32[]{:S(2)}) %all-to-all-start.2) | async-done | bytes 8388640 | tf_op jit(solution)/shard_map/all_to_all | solution.py:22
  668.8 12.0 %shard_map.139 = bf16[16,128,2048]{2,1,0:T(8,128)(2,1)} custom-call(bf16[8,16,128,256]{3,2,1,0:T(8,128)(2,1)} %all-to-all-done.2.in_ref), custom_call_target="tpu_custom_call" | custom-call | bytes 16777216 | tf_op jit(solution)/shard_map/pallas_call | solution.py:82
  (15 shorter events, 3.5 us)
Async XLA Ops:
  7.2 16.5 %copy-start.2 = (f32[256]{0:T(256)S(1)}, f32[256]{0:T(256)}, u32[]{:S(2)}) copy-start(f32[256]{0:T(256)} %param.15) | copy-start | bytes 3076
  7.2 16.5 %copy-start.1 = (f32[256,16]{0,1:T(8,128)S(1)}, f32[256,16]{0,1:T(8,128)}, u32[]{:S(2)}) copy-start(f32[256,16]{0,1:T(8,128)} %param.14) | copy-start | bytes 49156
  7.2 74.1 %all-reduce.4.cloned.1.call-start = ((), (), s32[]{:S(2)}) async-start(), calls=%async_computation.3 | async-start | bytes 131072 | tf_op jit(solution)/shard_map/psum | solution.py:96
  99.8 191.3 %all-to-all-start = ((bf16[8,16,256,128]{3,2,1,0:T(8,128)(2,1)}), bf16[8,16,256,128]{3,2,1,0:T(8,128)(2,1)}, u32[]{:S(2)}, u32[]{:S(2)}) async-start(bf16[8,16,256,128]{3,2,1,0:T(8,128)(2,1)} %shard_map.136), calls=%async_computation | async-start | bytes 16777216 | tf_op jit(solution)/shard_map/all_to_all | solution.py:22
  104.7 84.3 %all-reduce.6.cloned.1.call-start = ((), (), s32[]{:S(2)}) async-start(), calls=%async_computation.4 | async-start | bytes 262144 | tf_op jit(solution)/shard_map/psum | solution.py:102
  207.5 88.6 %copy-start = (f32[16,1024]{1,0:T(8,128)S(1)}, f32[16,1024]{1,0:T(8,128)}, u32[]{:S(2)}) copy-start(f32[16,1024]{1,0:T(8,128)} %get-tuple-element.19) | copy-start | bytes 196612
  291.0 188.9 %all-to-all-start.1 = ((bf16[8,16,256,128]{3,2,1,0:T(8,128)(2,1)}), bf16[8,16,256,128]{3,2,1,0:T(8,128)(2,1)}, u32[]{:S(2)}, u32[]{:S(2)}) async-start(bf16[8,16,256,128]{3,2,1,0:T(8,128)(2,1)} %shard_map.138), calls=%async_computation.1 | async-start | bytes 16777216 | tf_op jit(solution)/shard_map/all_to_all | solution.py:22
  479.9 188.8 %all-to-all-start.2 = ((bf16[8,16,128,256]{3,2,1,0:T(8,128)(2,1)}), bf16[8,16,128,256]{3,2,1,0:T(8,128)(2,1)}, u32[]{:S(2)}, u32[]{:S(2)}) async-start(bf16[8,16,128,256]{3,2,1,0:T(8,128)(2,1)} %bitcast.14), calls=%async_computation.2 | async-start | bytes 16777216 | tf_op jit(solution)/shard_map/all_to_all | solution.py:22
Sparse Core Ops, SparseCore 0:
  23.8 57.4 all-reduce.3
  131.1 57.8 all-reduce.5
